TPU v7x, 32 devices: a whole 2x2x4 slice. The times are simulated.
32 devices in a mesh: layer: 4 (over y, x), row: 2 (over core), col: 4 (over z).
Axes of the slice: x: 2, y: 2, z: 4, core: 2. Of those that a mesh axis runs over, the one named last changes fastest.
Arguments:
- block_values: bfloat16 [4, 2, 4, 32, 256, 256], P('layer', 'row', 'col'), may hold values from 0 to 3
- block_rows: int32 [4, 2, 4, 32], P('layer', 'row', 'col'), may hold values from 0 to 255
- block_cols: int32 [4, 2, 4, 32], P('layer', 'row', 'col'), may hold values from 0 to 127
- block_count: int32 [4, 2, 4], P('layer', 'row', 'col'), may hold values from 1 to 32, as said below
- dangling: int32 [4, 2, 4, 16384], P('layer', 'row', 'col'), may hold values 0 or 1
- start_ranks: float32 [4, 2, 4, 16384], P('layer', 'row', 'col'), may hold values from 0.2 to 5
Outputs:
- ranks: float32 [4, 2, 4, 16384], P('layer', 'row', 'col')
- residuals: float32 [3, 4], P(None, 'layer')
Inputs may be any that keep to these rules, and one draw needn't show every extreme that they name: `block_count`: live slots of a tile; in every layer some tile has all 32 slots live. `block_rows`: slots at or past a tile's count carry no edges; coordinates may repeat within a tile, and repeated blocks add.
All inputs are finite; a program needn't handle non-finite values. No bound on the sum of `dangling` on one device may be relied on, other than what follows from the above.
Results may differ from a plain program's by a relative error of at most 0.0012.
Values may be sent and summed in bfloat16 or wider, within the bound.
A program may use at most 64 MiB of HBM per device.

v0:
```python
import jax
import jax.numpy as jnp
from jax import lax
from jax.sharding import PartitionSpec as P

ITERS = 3


damping = 0.85
coupling = 0.3


def with_halo(x, sides, width):
    for axis, dim in sides:
        count, length = (lax.axis_size(axis), x.shape[dim])
        up = [(i, (i + 1) % count) for i in range(count - 1)]
        down = [(j, i) for i, j in up]
        last = lax.slice_in_dim(x, length - width, length, axis=dim)
        first = lax.slice_in_dim(x, 0, width, axis=dim)
        before = lax.ppermute(last, axis, up)
        after = lax.ppermute(first, axis, down)
        x = jnp.concatenate([before, x, after], axis=dim)
    return x


def block_terms(values, rows_here, cols_here, live_here, column_bf, row_blk):
    picked = jnp.take(column_bf, cols_here, axis=0)
    products = jnp.einsum("sij,sj->si", values, picked, preferred_element_type=jnp.float32)
    onehot = (rows_here[:, None] == jnp.arange(row_blk)[None, :]).astype(jnp.float32) * live_here[
        :, None
    ]
    return jnp.einsum("sb,si->bi", onehot, products, precision=lax.Precision.HIGHEST)


def layer_walk(values, rows_here, cols_here, live_here, column_bf, row_blk):
    return block_terms(values, rows_here, cols_here, live_here, column_bf, row_blk)


def local(block_values, block_rows, block_cols, block_count, dangling, start_ranks):
    layer_dev = start_ranks.shape[0]
    span_len = start_ranks.shape[-1]
    row_devices = lax.axis_size("row")
    col_devices = lax.axis_size("col")
    block_edge = block_values.shape[-1]
    slots = block_values.shape[3]
    col_blk = row_devices * span_len // block_edge
    row_blk = col_devices * span_len // block_edge
    node_total = row_devices * col_devices * span_len
    layers = layer_dev * lax.axis_size("layer")
    values = block_values[:, 0, 0]
    block_row = block_rows[:, 0, 0]
    block_col = block_cols[:, 0, 0]
    counts = block_count[:, 0, 0]
    live_slot = (jnp.arange(slots)[None, :] < counts[:, None]).astype(jnp.float32)
    colsum = jnp.einsum(
        "lsij,i->lsj",
        values,
        jnp.ones((block_edge,), jnp.bfloat16),
        preferred_element_type=jnp.float32,
    )
    onehot = (block_col[..., None] == jnp.arange(col_blk)[None, None, :]).astype(
        jnp.float32
    ) * live_slot[..., None]
    deg_part = jnp.einsum("lsb,lsj->lbj", onehot, colsum, precision=lax.Precision.HIGHEST)
    deg_part = deg_part.reshape(layer_dev, row_devices, 1, span_len)
    degree = lax.psum(deg_part, "row")
    own_degree = lax.dynamic_slice_in_dim(degree, lax.axis_index("row"), 1, 1)
    keep_mask = 1.0 - dangling.astype(jnp.float32)
    own_denominator = keep_mask * own_degree + 1.0
    layer_ids = lax.axis_index("layer") * layer_dev + jnp.arange(layer_dev)
    spread = (
        jnp.where((layer_ids == 0) | (layer_ids == layers - 1), 1.0, 0.5).astype(jnp.float32)
        * coupling
    )
    spread = spread.reshape(layer_dev, 1, 1, 1)
    ranks_now = start_ranks
    residual_list = []
    for iteration in range(ITERS):
        spill = ranks_now * spread
        padded = with_halo(spill.astype(jnp.bfloat16), (("layer", 0),), 1).astype(spill.dtype)
        arrive = padded[:-2] + padded[2:]
        scaled_own = (ranks_now * keep_mask / own_denominator).astype(jnp.bfloat16)
        column_vec = lax.all_gather(scaled_own, "row", axis=1, tiled=True)
        dangle_mass = lax.psum(jnp.sum(ranks_now / own_denominator, axis=(1, 2, 3)), ("row", "col"))
        scaled = column_vec.reshape(layer_dev, col_blk, block_edge)
        layer_terms = [
            layer_walk(values[0], block_row[0], block_col[0], live_slot[0], scaled[0], row_blk)
        ]
        partial_value = jnp.stack(layer_terms).reshape(layer_dev, 1, col_devices, span_len)
        whole = lax.psum(partial_value, "col")
        walk_sum = lax.dynamic_slice_in_dim(whole, lax.axis_index("col"), 1, 2)
        updated = damping * (
            (1.0 - coupling) * (walk_sum + dangle_mass.reshape(layer_dev, 1, 1, 1) / node_total)
            + arrive
        ) + (1.0 - damping)
        change = jnp.sum(jnp.abs(updated - ranks_now), axis=(1, 2, 3))
        change_total = lax.psum(change, ("row", "col"))
        residual_list.append(change_total)
        ranks_now = updated
    return (ranks_now, jnp.stack(residual_list))


def solution(mesh):
    placed = (
        P("layer", "row", "col", None, None, None),
        P("layer", "row", "col", None),
        P("layer", "row", "col", None),
        P("layer", "row", "col"),
        P("layer", "row", "col", None),
        P("layer", "row", "col", None),
    )
    return jax.shard_map(
        local,
        mesh=mesh,
        in_specs=placed,
        out_specs=(P("layer", "row", "col", None), P(None, "layer")),
        check_vma=False,
    )
```

profile of v0, /device:TPU:0, one launch (start us, length us, event | category | flops | bytes accessed | tf_op | source)
XLA Modules:
  0.0 197.4 jit_solution(1086443442296965706)
XLA Ops:
  7.2 0.0 copy-start.3
  7.2 0.0 copy-start
  7.2 0.0 copy-start.1
  7.2 0.0 all-reduce.6.cloned.1.call-start
  7.9 0.0 copy-start.2
  7.9 2.8 %fusion.6 = f32[1,32,256]{2,0,1:T(1,128)S(1)} fusion(bf16[1,1,1,32,256,256]{5,4,3,2,1,0:T(8,128)(2,1)} %param.8), kind=kOutput, calls=%fused_computation.9 | convolution fusion | flops 4194304 | bytes 4227072 | tf_op jit(solution)/shard_map/lsij,i->lsj/dot_general | solution.py:55
  10.8 0.4 fusion.33
  11.2 0.8 reshape.291
  12.0 0.0 all-reduce.6.cloned.1.call-update
  12.0 0.0 all-reduce.8.cloned.1.call-start
  12.1 20.7 %all-reduce.6.cloned.1.call-done = f32[1,2,1,16384]{3,2,0,1:T(1,128)} async-done(((f32[1,2,1,16384]{3,2,0,1:T(1,128)}), f32[1,2,1,16384]{3,2,0,1:T(1,128)}) %all-reduce.6.cloned.1.call-update) | async-done | bytes 131088 | tf_op jit(solution)/shard_map/psum | solution.py:66
  32.8 1.6 fusion.20
  34.4 0.1 fusion.23
  34.5 1.9 all_gather.9
  36.4 0.4 reduce.6
  36.9 0.6 gather_fusion
  37.5 0.1 select_bitcast_fusion.2
  37.6 3.4 %fusion.4 = f32[32,1,256]{2,1,0:T(1,128)S(1)} fusion(bf16[1,1,1,32,256,256]{5,4,3,2,1,0:T(8,128)(2,1)} %param.8, bf16[32,256,1]{1,0,2:T(8,128)(2,1)S(1)} %select_bitcast_fusion.2), kind=kOutput, calls=%fused_computation.7 | convolution fusion | flops 4194304 | bytes 4243456 | tf_op jit(solution)/shard_map/sij,sj->si/dot_general | solution.py:28
  40.9 0.5 fusion.28
  41.5 0.8 reshape_stack.9
  42.3 0.0 all-reduce.8.cloned.1.call-update
  42.3 0.0 all-reduce.10.cloned.1.call-start
  42.4 3.7 %collective-permute-start = (bf16[1,1,1,16384]{3,2,0,1:T(2,128)(2,1)S(1)}, bf16[1,1,1,16384]{3,2,0,1:T(2,128)(2,1)S(1)}, u32[]{:S(2)}, u32[]{:S(2)}) collective-permute-start(bf16[1,1,1,16384]{3,2,0,1:T(2,128)(2,1)S(1)} %bitcast_convert_fusion), channel_id=1, source_target_pairs={{0,8},{8,16},{16,24},{1,9},{9,17},{17,25},{2,10},{10,18},{18,26},{... | collective-permute-start | bytes 98312 | tf_op jit(solution)/shard_map/ppermute | solution.py:20
  46.1 1.3 collective-permute-start.1
  47.4 17.4 %psum.72 = f32[1]{0:T(128)} all-reduce(f32[1]{0:T(128)} %bitcast.11), channel_id=1, replica_groups=mesh['layer'=4,'row'=2,'col'=4] {'row','col'}, use_global_device_ids=true, to_apply=%region_3.5 | all-reduce | flops 1 | bytes 8 | tf_op jit(solution)/shard_map/psum | solution.py:84
  65.5 0.0 collective-permute-done
  65.5 0.0 collective-permute-done.1
  65.5 13.6 %all-reduce.8.cloned.1.call-done = f32[1,1,4,16384]{3,2,0,1:T(4,128)} async-done(((f32[1,1,4,16384]{3,2,0,1:T(4,128)}), f32[1,1,4,16384]{3,2,0,1:T(4,128)}) %all-reduce.8.cloned.1.call-update) | async-done | bytes 262160 | tf_op jit(solution)/shard_map/psum | solution.py:90
  79.1 1.8 divide_reduce_fusion.1
  81.0 0.1 fusion.21
  81.1 1.9 all_gather.10
  83.0 0.4 reduce.7
  83.5 0.6 gather_fusion.1
  84.1 0.1 select_bitcast_fusion.1
  84.2 3.4 %fusion.2 = f32[32,1,256]{2,1,0:T(1,128)S(1)} fusion(bf16[1,1,1,32,256,256]{5,4,3,2,1,0:T(8,128)(2,1)} %param.8, bf16[32,256,1]{1,0,2:T(8,128)(2,1)S(1)} %select_bitcast_fusion.1), kind=kOutput, calls=%fused_computation.5 | convolution fusion | flops 4194304 | bytes 4243456 | tf_op jit(solution)/shard_map/sij,sj->si/dot_general | solution.py:28
  87.6 0.5 fusion.26
  88.1 0.8 reshape_stack.10
  88.9 0.0 all-reduce.10.cloned.1.call-update
  88.9 0.0 all-reduce.12.cloned.1.call-start
  89.0 3.4 %collective-permute-start.2 = (bf16[1,1,1,16384]{3,2,0,1:T(2,128)(2,1)S(1)}, bf16[1,1,1,16384]{3,2,0,1:T(2,128)(2,1)S(1)}, u32[]{:S(2)}, u32[]{:S(2)}) collective-permute-start(bf16[1,1,1,16384]{3,2,0,1:T(2,128)(2,1)S(1)} %get-tuple-element.23), channel_id=1, source_target_pairs={{0,8},{8,16},{16,24},{1,9},{9,17},{17,25},{2,10},{10,18},{18,26},{... | collective-permute-start | bytes 98312 | tf_op jit(solution)/shard_map/ppermute | solution.py:20
  92.4 1.3 collective-permute-start.3
  93.7 16.5 %psum.74 = f32[1]{0:T(128)} all-reduce(f32[1]{0:T(128)} %bitcast.18), channel_id=1, replica_groups=mesh['layer'=4,'row'=2,'col'=4] {'row','col'}, use_global_device_ids=true, to_apply=%region_6.8 | all-reduce | flops 1 | bytes 8 | tf_op jit(solution)/shard_map/psum | solution.py:84
  110.8 0.0 collective-permute-done.2
  110.8 0.0 collective-permute-done.3
  110.8 13.7 %all-reduce.10.cloned.1.call-done = f32[1,1,4,16384]{3,2,0,1:T(4,128)} async-done(((f32[1,1,4,16384]{3,2,0,1:T(4,128)}), f32[1,1,4,16384]{3,2,0,1:T(4,128)}) %all-reduce.10.cloned.1.call-update) | async-done | bytes 262160 | tf_op jit(solution)/shard_map/psum | solution.py:90
  124.6 1.8 divide_reduce_fusion
  126.4 0.1 fusion.22
  126.5 1.9 all_gather.11
  128.4 0.4 reduce.8
  128.9 0.6 gather_fusion.2
  129.5 0.1 select_bitcast_fusion
  129.6 3.4 %fusion = f32[32,1,256]{2,1,0:T(1,128)S(1)} fusion(bf16[1,1,1,32,256,256]{5,4,3,2,1,0:T(8,128)(2,1)} %param.8, bf16[32,256,1]{1,0,2:T(8,128)(2,1)S(1)} %select_bitcast_fusion), kind=kOutput, calls=%fused_computation.3 | convolution fusion | flops 4194304 | bytes 4243456 | tf_op jit(solution)/shard_map/sij,sj->si/dot_general | solution.py:28
  133.0 0.5 fusion.24
  133.5 0.8 reshape_stack.11
  134.3 0.0 all-reduce.12.cloned.1.call-update
  134.3 3.4 %collective-permute-start.4 = (bf16[1,1,1,16384]{3,2,0,1:T(2,128)(2,1)S(1)}, bf16[1,1,1,16384]{3,2,0,1:T(2,128)(2,1)S(1)}, u32[]{:S(2)}, u32[]{:S(2)}) collective-permute-start(bf16[1,1,1,16384]{3,2,0,1:T(2,128)(2,1)S(1)} %get-tuple-element.21), channel_id=1, source_target_pairs={{0,8},{8,16},{16,24},{1,9},{9,17},{17,25},{2,10},{10,18},{18,26},{... | collective-permute-start | bytes 98312 | tf_op jit(solution)/shard_map/ppermute | solution.py:20
  137.7 1.3 collective-permute-start.5
  139.0 16.4 %psum.76 = f32[1]{0:T(128)} all-reduce(f32[1]{0:T(128)} %bitcast.23), channel_id=1, replica_groups=mesh['layer'=4,'row'=2,'col'=4] {'row','col'}, use_global_device_ids=true, to_apply=%region_9.11 | all-reduce | flops 1 | bytes 8 | tf_op jit(solution)/shard_map/psum | solution.py:84
  156.1 0.0 collective-permute-done.4
  156.1 0.0 collective-permute-done.5
  156.1 13.8 %all-reduce.12.cloned.1.call-done = f32[1,1,4,16384]{3,2,0,1:T(4,128)} async-done(((f32[1,1,4,16384]{3,2,0,1:T(4,128)}), f32[1,1,4,16384]{3,2,0,1:T(4,128)}) %all-reduce.12.cloned.1.call-update) | async-done | bytes 262160 | tf_op jit(solution)/shard_map/psum | solution.py:90
  170.0 2.6 %fusion.19 = (f32[]{:T(128)}, f32[]{:T(128)}, f32[]{:T(128)}, f32[1,1,1,16384]{3,2,0,1:T(1,128)}) fusion(f32[1,1,1,16384]{3,2,0,1:T(1,128)S(1)} %get-tuple-element.17, f32[1,1,1,16384]{3,2,1,0:T(1,128)S(1)} %copy-done.1, f32[1,1,1,16384]{3,2,0,1:T(1,128)S(1)} %get-tuple-element.15, bf16[1,1,1,16384]{3,2,0,1:T(2,128)(2,1)S(1)} %collective-permute-done.5, ...), kind=kLoop, calls=%fused_computation.43 | loop fusion | flops 344061 | bytes 426004 | tf_op jit(solution)/shard_map/reduce_sum | solution.py:96
  172.6 15.8 %all-reduce = (f32[1,1]{0,1:T(1,128)}, f32[1,1]{0,1:T(1,128)}, f32[1,1]{0,1:T(1,128)}) all-reduce(f32[1,1]{0,1:T(1,128)} %bitcast.29, f32[1,1]{0,1:T(1,128)} %bitcast.28, f32[1,1]{0,1:T(1,128)} %bitcast.27), channel_id=1, replica_groups=mesh['layer'=4,'row'=2,'col'=4] {'row','col'}, use_global_device_ids=true, to_apply=%region_15.17 | all-reduce | flops 3 | bytes 24 | tf_op jit(solution)/shard_map/psum | solution.py:97
  188.4 2.5 %pad_maximum_fusion.6 = f32[3,1]{0,1:T(1,128)} fusion(f32[1,1]{0,1:T(1,128)} %get-tuple-element.10, f32[1,1]{0,1:T(1,128)} %get-tuple-element.11, f32[1,1]{0,1:T(1,128)} %get-tuple-element.12), kind=kLoop, calls=%fused_computation.90 | loop fusion | flops 6 | bytes 24 | tf_op jit(solution)/shard_map/stack | solution.py:100
  (12 shorter events, 0.2 us)
Async XLA Ops:
  7.2 3.6 %copy-start.3 = (s32[1,1,1,32]{3,2,1,0:T(1,128)S(1)}, s32[1,1,1,32]{3,2,1,0:T(1,128)}, u32[]{:S(2)}) copy-start(s32[1,1,1,32]{3,2,1,0:T(1,128)} %param.10) | copy-start | bytes 388
  7.2 25.6 %copy-start = (s32[1,1,1,16384]{3,2,1,0:T(1,128)S(1)}, s32[1,1,1,16384]{3,2,1,0:T(1,128)}, u32[]{:S(2)}) copy-start(s32[1,1,1,16384]{3,2,1,0:T(1,128)} %param.12) | copy-start | bytes 196612
  7.2 25.6 %copy-start.1 = (f32[1,1,1,16384]{3,2,1,0:T(1,128)S(1)}, f32[1,1,1,16384]{3,2,1,0:T(1,128)}, u32[]{:S(2)}) copy-start(f32[1,1,1,16384]{3,2,1,0:T(1,128)} %param.13) | copy-start | bytes 196612
  7.2 25.6 %all-reduce.6.cloned.1.call-start = ((), (), s32[]{:S(2)}) async-start(), calls=%async_computation | async-start | bytes 262144 | tf_op jit(solution)/shard_map/psum | solution.py:66
  7.9 33.0 %copy-start.2 = (s32[1,1,1,32]{3,2,1,0:T(1,128)S(1)}, s32[1,1,1,32]{3,2,1,0:T(1,128)}, u32[]{:S(2)}) copy-start(s32[1,1,1,32]{3,2,1,0:T(1,128)} %param.9) | copy-start | bytes 388
  12.0 67.2 %all-reduce.8.cloned.1.call-start = ((), (), s32[]{:S(2)}) async-start(), calls=%async_computation.1 | async-start | bytes 524288 | tf_op jit(solution)/shard_map/psum | solution.py:90
  42.3 82.3 %all-reduce.10.cloned.1.call-start = ((), (), s32[]{:S(2)}) async-start(), calls=%async_computation.2 | async-start | bytes 524288 | tf_op jit(solution)/shard_map/psum | solution.py:90
  42.4 23.1 %collective-permute-start = (bf16[1,1,1,16384]{3,2,0,1:T(2,128)(2,1)S(1)}, bf16[1,1,1,16384]{3,2,0,1:T(2,128)(2,1)S(1)}, u32[]{:S(2)}, u32[]{:S(2)}) collective-permute-start(bf16[1,1,1,16384]{3,2,0,1:T(2,128)(2,1)S(1)} %bitcast_convert_fusion), channel_id=1, source_target_pairs={{0,8},{8,16},{16,24},{1,9},{9,17},{17,25},{2,10},{10,18},{18,26},{... | collective-permute-start | bytes 98312 | tf_op jit(solution)/shard_map/ppermute | solution.py:20
  46.1 19.4 %collective-permute-start.1 = (bf16[1,1,1,16384]{3,2,0,1:T(2,128)(2,1)S(1)}, bf16[1,1,1,16384]{3,2,0,1:T(2,128)(2,1)S(1)}, u32[]{:S(2)}, u32[]{:S(2)}) collective-permute-start(bf16[1,1,1,16384]{3,2,0,1:T(2,128)(2,1)S(1)} %bitcast_convert_fusion), channel_id=1, source_target_pairs={{8,0},{16,8},{24,16},{9,1},{17,9},{25,17},{10,2},{18,10},{26,18},{... | collective-permute-start | bytes 98312 | tf_op jit(solution)/shard_map/ppermute | solution.py:21
  88.9 81.0 %all-reduce.12.cloned.1.call-start = ((), (), s32[]{:S(2)}) async-start(), calls=%async_computation.3 | async-start | bytes 524288 | tf_op jit(solution)/shard_map/psum | solution.py:90
  89.0 21.8 %collective-permute-start.2 = (bf16[1,1,1,16384]{3,2,0,1:T(2,128)(2,1)S(1)}, bf16[1,1,1,16384]{3,2,0,1:T(2,128)(2,1)S(1)}, u32[]{:S(2)}, u32[]{:S(2)}) collective-permute-start(bf16[1,1,1,16384]{3,2,0,1:T(2,128)(2,1)S(1)} %get-tuple-element.23), channel_id=1, source_target_pairs={{0,8},{8,16},{16,24},{1,9},{9,17},{17,25},{2,10},{10,18},{18,26},{... | collective-permute-start | bytes 98312 | tf_op jit(solution)/shard_map/ppermute | solution.py:20
  92.4 18.4 %collective-permute-start.3 = (bf16[1,1,1,16384]{3,2,0,1:T(2,128)(2,1)S(1)}, bf16[1,1,1,16384]{3,2,0,1:T(2,128)(2,1)S(1)}, u32[]{:S(2)}, u32[]{:S(2)}) collective-permute-start(bf16[1,1,1,16384]{3,2,0,1:T(2,128)(2,1)S(1)} %get-tuple-element.23), channel_id=1, source_target_pairs={{8,0},{16,8},{24,16},{9,1},{17,9},{25,17},{10,2},{18,10},{26,18},{... | collective-permute-start | bytes 98312 | tf_op jit(solution)/shard_map/ppermute | solution.py:21
  134.3 21.8 %collective-permute-start.4 = (bf16[1,1,1,16384]{3,2,0,1:T(2,128)(2,1)S(1)}, bf16[1,1,1,16384]{3,2,0,1:T(2,128)(2,1)S(1)}, u32[]{:S(2)}, u32[]{:S(2)}) collective-permute-start(bf16[1,1,1,16384]{3,2,0,1:T(2,128)(2,1)S(1)} %get-tuple-element.21), channel_id=1, source_target_pairs={{0,8},{8,16},{16,24},{1,9},{9,17},{17,25},{2,10},{10,18},{18,26},{... | collective-permute-start | bytes 98312 | tf_op jit(solution)/shard_map/ppermute | solution.py:20
  137.7 18.4 %collective-permute-start.5 = (bf16[1,1,1,16384]{3,2,0,1:T(2,128)(2,1)S(1)}, bf16[1,1,1,16384]{3,2,0,1:T(2,128)(2,1)S(1)}, u32[]{:S(2)}, u32[]{:S(2)}) collective-permute-start(bf16[1,1,1,16384]{3,2,0,1:T(2,128)(2,1)S(1)} %get-tuple-element.21), channel_id=1, source_target_pairs={{8,0},{16,8},{24,16},{9,1},{17,9},{25,17},{10,2},{18,10},{26,18},{... | collective-permute-start | bytes 98312 | tf_op jit(solution)/shard_map/ppermute | solution.py:21
Sparse Core Ops, SparseCore 0:
  12.1 20.6 all-reduce.5
  42.4 36.6 all-reduce.7
  89.1 35.4 all-reduce.9
  134.5 35.4 all-reduce.11
where the time goes:
time: 199 us; the launch traced here: 197 us
  blocking collectives  71.9 us (36%)
  waiting for transfers between devices  62 us (31%)
  between operations  16.7 us (8%)
  matrix products  14.8 us (7%)
  starting transfers between devices  14.5 us (7%)
  other arithmetic  12.3 us (6%)
  local copies, waits for them, and re-layouts  5.32 us (3%)
    psum x3, blocking collectives, local(): lax.psum(jnp.sum(ranks_now / own_denominator, axis=(1, 2, 3)), ('row', 'c...  50.4 us
    psum x3, waiting for transfers between devices, local(): whole = lax.psum(partial_value, 'col')  41.2 us
    psum x1, waiting for transfers between devices, local(): degree = lax.psum(deg_part, 'row')  20.7 us
    psum x1, blocking collectives, local(): change_total = lax.psum(change, ('row', 'col'))  15.8 us
    ppermute x3, starting transfers between devices, with_halo(): before = lax.ppermute(last, axis, up)  10.4 us
    dot_general x3, matrix products, block_terms(): jnp.einsum('sij,sj->si', values, picked, preferred_element_type=jnp.float32)  10.1 us
    all_gather x3, blocking collectives, local(): column_vec = lax.all_gather(scaled_own, 'row', axis=1, tiled=True)  5.7 us
    reduce_sum x3, other arithmetic, local(): jnp.sum(ranks_now / own_denominator, axis=(1, 2, 3))  5.25 us
  transfers between devices with their start and end apart: 10, of which 4 were waited for; matrix products, arithmetic and copies ran while one was open for 0% of the time, Pallas kernels for 0%

commit v1 on v0

v1 whole, which is shorter than its diff:
```python
import functools

import jax
import jax.numpy as jnp
from jax import lax
from jax.experimental import pallas as pl
from jax.experimental.pallas import tpu as pltpu
from jax.sharding import PartitionSpec as P

ITERS = 3
CHUNK = 16

damping = 0.85
coupling = 0.3


def fold(v):
    rows, lanes = v.shape
    acc = v[:, 0:128]
    for h in range(1, lanes // 128):
        acc = acc + v[:, h * 128 : (h + 1) * 128]
    return jnp.sum(acc.reshape(rows // 8, 8, 128), axis=0)


def split(v):
    hi = v.astype(jnp.bfloat16)
    lo = (v - hi.astype(jnp.float32)).astype(jnp.bfloat16)
    return hi, lo


def dot(a, b):
    return jnp.dot(a, b, preferred_element_type=jnp.float32)


def kernel(
    nl, nr, nc, nodes,
    values_hbm, rows_ref, cols_ref, count_ref, dang_hbm, start_hbm,
    ranks_hbm, resid_ref,
    values, dang_in, start_in, out_buf, x_ref, inv_ref, kinv_ref, keep_ref,
    colsum, ohrow, ohcol, own_prod, chg,
    deg_send, deg_recv, row_send, row_recv,
    sc_send, sc_recv, ma_send, ma_recv, mb_send, mb_recv,
    pr_send, pr_recv, sp_send, sp_recv, rs_send, rs_recv,
    sem_in, sem_v,
    deg_ss, deg_rs, row_ss, row_rs, sc_ss, sc_rs, ma_ss, ma_rs, mb_ss, mb_rs,
    pr_ss, pr_rs, sp_ss, sp_rs, rs_ss, rs_rs,
):
    l, r, c = (lax.axis_index(a) for a in ("layer", "row", "col"))
    slots, edge, _ = values.shape
    blocks = x_ref.shape[0]
    halves = edge // 128
    nchunk = slots // CHUNK
    f32, bf16 = jnp.float32, jnp.bfloat16

    def remote(src, dst, ss, rs, ll, rr, cc):
        return pltpu.make_async_remote_copy(
            src_ref=src, dst_ref=dst, send_sem=ss, recv_sem=rs,
            device_id=(ll, rr, cc), device_id_type=pl.DeviceIdType.MESH,
        )

    in_d = pltpu.make_async_copy(dang_hbm, dang_in, sem_in.at[0])
    in_x = pltpu.make_async_copy(start_hbm, start_in, sem_in.at[1])
    vcopies = [
        pltpu.make_async_copy(
            values_hbm.at[pl.ds(k * CHUNK, CHUNK)], values.at[pl.ds(k * CHUNK, CHUNK)], sem_v.at[k]
        )
        for k in range(nchunk)
    ]
    for cp in vcopies:
        cp.start()
    in_x.start()
    in_d.start()

    peers = [(dr, dc) for dr in range(nr) for dc in range(nc) if (dr, dc) != (0, 0)]
    barrier = pltpu.get_barrier_semaphore()
    for dr, dc in peers:
        pl.semaphore_signal(
            barrier, inc=1,
            device_id=(l, lax.rem(r + dr, nr), lax.rem(c + dc, nc)),
            device_id_type=pl.DeviceIdType.MESH,
        )

    @pl.when(l > 0)
    def _():
        pl.semaphore_signal(
            barrier, inc=1, device_id=(l - 1, r, c), device_id_type=pl.DeviceIdType.MESH)

    @pl.when(l < nl - 1)
    def _():
        pl.semaphore_signal(
            barrier, inc=1, device_id=(l + 1, r, c), device_id_type=pl.DeviceIdType.MESH)

    live = lax.broadcasted_iota(jnp.int32, (1, slots), 1) < count_ref[0]
    rows = jnp.where(live, rows_ref[...], -1)
    cols = jnp.where(live, cols_ref[...], -1)
    row_send[...] = jnp.broadcast_to(
        jnp.concatenate([rows, jnp.full((1, 128 - slots), -1, jnp.int32)], axis=1), (8, 128)
    ).astype(f32)

    eye = lax.broadcasted_iota(jnp.int32, (slots, slots), 0) == lax.broadcasted_iota(
        jnp.int32, (slots, slots), 1)
    colv = jnp.sum(
        jnp.where(eye, jnp.broadcast_to(cols_ref[...], (slots, slots)).astype(f32), 0.0),
        axis=1, keepdims=True,
    )
    for d in range(nr):
        base = lax.rem(r - d + nr, nr) * blocks
        at = (lax.broadcasted_iota(jnp.int32, (slots, blocks), 1) + base).astype(f32)
        ohcol[d] = jnp.where(colv == at, 1.0, 0.0).astype(bf16)

    ones = jnp.ones((CHUNK, edge), bf16)
    rid = lax.broadcasted_iota(jnp.int32, (CHUNK, edge), 0)
    for k in range(nchunk):
        vcopies[k].wait()
        acc = jnp.zeros((CHUNK, edge), f32)
        for s in range(CHUNK):
            acc = jnp.where(rid == s, dot(ones, values[k * CHUNK + s]), acc)
        colsum[k * CHUNK : (k + 1) * CHUNK] = acc

    in_x.wait()
    in_d.wait()
    for h in range(halves):
        x_ref[:, h * 128 : (h + 1) * 128] = start_in[pl.ds(h, blocks, stride=halves), :]
        keep_ref[:, h * 128 : (h + 1) * 128] = 1.0 - dang_in[
            pl.ds(h, blocks, stride=halves), :].astype(f32)

    hi, lo = split(colsum[...])

    def deg_of(rr):
        base = rr * blocks
        at = lax.broadcasted_iota(jnp.int32, (blocks, slots), 0) + base
        oh = jnp.where(jnp.broadcast_to(cols, (blocks, slots)) == at, 1.0, 0.0).astype(bf16)
        return dot(oh, hi) + dot(oh, lo)

    for d in range(1, nr):
        deg_send[d] = deg_of(lax.rem(r + d, nr))

    pl.semaphore_wait(
        barrier, len(peers) + (l > 0).astype(jnp.int32) + (l < nl - 1).astype(jnp.int32))

    pre = []
    for d in range(1, nr):
        pre.append(remote(deg_send.at[d], deg_recv.at[d], deg_ss.at[d], deg_rs.at[d],
                          l, lax.rem(r + d, nr), c))
    for d in range(1, nc):
        pre.append(remote(row_send, row_recv.at[d], row_ss.at[d], row_rs.at[d],
                          l, r, lax.rem(c + d, nc)))
    for cp in pre:
        cp.start()

    def spill_copies(t):
        return (
            remote(sp_send.at[t], sp_recv.at[t, 0], sp_ss.at[t, 0], sp_rs.at[t, 0], l + 1, r, c),
            remote(sp_send.at[t], sp_recv.at[t, 1], sp_ss.at[t, 1], sp_rs.at[t, 1], l - 1, r, c),
        )

    spread = jnp.where((l == 0) | (l == nl - 1), 1.0, 0.5).astype(f32) * coupling

    def send_spill(t, x):
        sp_send[t] = (x * spread).astype(sp_send.dtype)
        up, down = spill_copies(t)

        @pl.when(l < nl - 1)
        def _():
            up.start()

        @pl.when(l > 0)
        def _():
            down.start()

    @pl.when(l == 0)
    def _():
        for t in range(ITERS):
            sp_recv[t, 0] = jnp.zeros((blocks, edge), sp_recv.dtype)

    @pl.when(l == nl - 1)
    def _():
        for t in range(ITERS):
            sp_recv[t, 1] = jnp.zeros((blocks, edge), sp_recv.dtype)

    send_spill(0, x_ref[...])

    deg = deg_of(r)
    for d in range(1, nr):
        pre[d - 1].wait_recv()
        deg = deg + deg_recv[d]
    keep = keep_ref[...]
    inv = 1.0 / (keep * deg + 1.0)
    inv_ref[...] = inv
    kinv_ref[...] = keep * inv

    def row_onehot(tab):
        at = (lax.broadcasted_iota(jnp.int32, (blocks, slots), 0) + c * blocks).astype(f32)
        return jnp.where(jnp.broadcast_to(tab[0:1, 0:slots], (blocks, slots)) == at,
                         1.0, 0.0).astype(bf16)

    chg[...] = jnp.zeros((8, 128), f32)

    def step(t, _):
        x = x_ref[...]
        scaled = (x * kinv_ref[...]).astype(bf16)
        sc_send[t] = scaled
        sc = [
            remote(sc_send.at[t], sc_recv.at[t, d], sc_ss.at[t, d], sc_rs.at[t, d],
                   l, lax.rem(r + d, nr), c)
            for d in range(1, nr)
        ]
        for cp in sc:
            cp.start()
        mass_own = fold(x * inv_ref[...])
        ma_send[t] = mass_own
        ma = [
            remote(ma_send.at[t], ma_recv.at[t, d], ma_ss.at[t, d], ma_rs.at[t, d],
                   l, lax.rem(r + d, nr), c)
            for d in range(1, nr)
        ]
        for cp in ma:
            cp.start()

        @pl.when(t > 0)
        def _():
            send_spill(t, x_ref[...])

        picked = dot(ohcol[0], scaled)
        for d in range(1, nr):
            sc[d - 1].wait_recv()
            picked = picked + dot(ohcol[d], sc_recv[t, d])
        picked = picked.astype(bf16)

        pr = []
        for k in range(nchunk):
            lhs = picked[k * CHUNK : (k + 1) * CHUNK]
            acc = jnp.zeros((CHUNK, edge), f32)
            for s in range(CHUNK):
                res = lax.dot_general(
                    lhs, values[k * CHUNK + s], (((1,), (1,)), ((), ())),
                    preferred_element_type=f32)
                acc = jnp.where(rid == s, res, acc)
            own_prod[k * CHUNK : (k + 1) * CHUNK] = acc
            pr_send[t, k] = acc.astype(pr_send.dtype)
            for d in range(1, nc):
                cp = remote(pr_send.at[t, k], pr_recv.at[t, d, k], pr_ss.at[t, d, k],
                            pr_rs.at[t, d, k], l, r, lax.rem(c + d, nc))
                cp.start()
                pr.append((d, k, cp))

        mass_row = mass_own
        for d in range(1, nr):
            ma[d - 1].wait_recv()
            mass_row = mass_row + ma_recv[t, d]
        mb_send[t] = mass_row
        mb = [
            remote(mb_send.at[t], mb_recv.at[t, d], mb_ss.at[t, d], mb_rs.at[t, d],
                   l, r, lax.rem(c + d, nc))
            for d in range(1, nc)
        ]
        for cp in mb:
            cp.start()

        @pl.when(t == 0)
        def _():
            ohrow[0] = row_onehot(row_send)
            for d in range(1, nc):
                pre[nr - 1 + d - 1].wait_recv()
                ohrow[d] = row_onehot(row_recv[d])

        phi, plo = split(own_prod[...])
        walk = dot(ohrow[0], phi) + dot(ohrow[0], plo)

        up, down = spill_copies(t)

        @pl.when(l > 0)
        def _():
            up.wait_recv()

        @pl.when(l < nl - 1)
        def _():
            down.wait_recv()

        arrive = sp_recv[t, 0].astype(f32) + sp_recv[t, 1].astype(f32)
        mass = mass_row
        for d in range(1, nc):
            mb[d - 1].wait_recv()
            mass = mass + mb_recv[t, d]
        rest = damping * ((1.0 - coupling) * (jnp.sum(mass) / nodes) + arrive) + (1.0 - damping)

        for d, k, cp in pr:
            cp.wait_recv()
        for d in range(1, nc):
            got = pr_recv[t, d].reshape(slots, edge)
            if got.dtype == bf16:
                walk = walk + dot(ohrow[d], got)
            else:
                ghi, glo = split(got)
                walk = walk + dot(ohrow[d], ghi) + dot(ohrow[d], glo)
        updated = damping * (1.0 - coupling) * walk + rest
        x_ref[...] = updated
        change = jnp.sum(fold(jnp.abs(updated - x)))
        lane = lax.broadcasted_iota(jnp.int32, (8, 128), 1)
        chg[...] = jnp.where(lane == t, change, chg[...])

        for cp in sc + ma + mb + [p[2] for p in pr]:
            cp.wait_send()

        @pl.when(l < nl - 1)
        def _():
            up.wait_send()

        @pl.when(l > 0)
        def _():
            down.wait_send()

        return 0

    lax.fori_loop(0, ITERS, step, 0)

    rs_send[...] = chg[0:1]
    rs = []
    for i, (dr, dc) in enumerate(peers):
        cp = remote(rs_send, rs_recv.at[i], rs_ss.at[i], rs_rs.at[i],
                    l, lax.rem(r + dr, nr), lax.rem(c + dc, nc))
        cp.start()
        rs.append(cp)
    for h in range(halves):
        out_buf[pl.ds(h, blocks, stride=halves), :] = x_ref[:, h * 128 : (h + 1) * 128]
    out = pltpu.make_async_copy(out_buf, ranks_hbm, sem_in.at[0])
    out.start()
    for cp in pre:
        cp.wait_send()
    total = rs_send[...]
    for i, cp in enumerate(rs):
        cp.wait_recv()
        total = total + rs_recv[i]
    pick = lax.broadcasted_iota(jnp.int32, (ITERS, 128), 0) == lax.broadcasted_iota(
        jnp.int32, (ITERS, 128), 1)
    resid_ref[...] = jnp.sum(
        jnp.where(pick, jnp.broadcast_to(total, (ITERS, 128)), 0.0), axis=1, keepdims=True)
    for cp in rs:
        cp.wait_send()
    out.wait()


def local(block_values, block_rows, block_cols, block_count, dangling, start_ranks):
    span = start_ranks.shape[-1]
    nl, nr, nc = (lax.axis_size(a) for a in ("layer", "row", "col"))
    slots, edge = block_values.shape[3], block_values.shape[-1]
    blocks = span // edge
    nchunk = slots // CHUNK
    nodes = nr * nc * span
    npeer = nr * nc - 1
    f32, bf16 = jnp.float32, jnp.bfloat16
    vm, dma = pltpu.VMEM, pltpu.SemaphoreType.DMA
    big = (blocks, edge)
    PT, ST = bf16, f32
    scratch = [
        vm((slots, edge, edge), bf16), vm((span // 128, 128), jnp.int32), vm((span // 128, 128), f32),
        vm((span // 128, 128), f32), vm(big, f32), vm(big, f32), vm(big, f32), vm(big, f32),
        vm((slots, edge), f32), vm((nc, blocks, slots), bf16), vm((nr, slots, blocks), bf16),
        vm((slots, edge), f32), vm((8, 128), f32),
        vm((nr,) + big, f32), vm((nr,) + big, f32), vm((8, 128), f32), vm((nc, 8, 128), f32),
        vm((ITERS,) + big, bf16), vm((ITERS, nr) + big, bf16),
        vm((ITERS, 8, 128), f32), vm((ITERS, nr, 8, 128), f32),
        vm((ITERS, 8, 128), f32), vm((ITERS, nc, 8, 128), f32),
        vm((ITERS, nchunk, CHUNK, edge), PT), vm((ITERS, nc, nchunk, CHUNK, edge), PT),
        vm((ITERS,) + big, ST), vm((ITERS, 2) + big, ST),
        vm((1, 128), f32), vm((npeer, 1, 128), f32),
        dma((2,)), dma((nchunk,)),
        dma((nr,)), dma((nr,)), dma((nc,)), dma((nc,)),
        dma((ITERS, nr)), dma((ITERS, nr)), dma((ITERS, nr)), dma((ITERS, nr)),
        dma((ITERS, nc)), dma((ITERS, nc)),
        dma((ITERS, nc, nchunk)), dma((ITERS, nc, nchunk)),
        dma((ITERS, 2)), dma((ITERS, 2)), dma((npeer,)), dma((npeer,)),
    ]
    hbm = pl.BlockSpec(memory_space=pl.ANY)
    vmem = pl.BlockSpec(memory_space=pltpu.VMEM)
    smem = pl.BlockSpec(memory_space=pltpu.SMEM)
    ranks, resid = pl.pallas_call(
        functools.partial(kernel, nl, nr, nc, nodes),
        out_shape=(
            jax.ShapeDtypeStruct((span // 128, 128), f32),
            jax.ShapeDtypeStruct((ITERS, 1), f32),
        ),
        in_specs=[hbm, vmem, vmem, smem, hbm, hbm],
        out_specs=(hbm, vmem),
        scratch_shapes=scratch,
        compiler_params=pltpu.CompilerParams(collective_id=0, has_side_effects=True),
    )(
        block_values.reshape(slots, edge, edge),
        block_rows.reshape(1, slots),
        block_cols.reshape(1, slots),
        block_count.reshape(1),
        dangling.reshape(span // 128, 128),
        start_ranks.reshape(span // 128, 128),
    )
    return ranks.reshape(1, 1, 1, span), resid


def solution(mesh):
    placed = (
        P("layer", "row", "col", None, None, None),
        P("layer", "row", "col", None),
        P("layer", "row", "col", None),
        P("layer", "row", "col"),
        P("layer", "row", "col", None),
        P("layer", "row", "col", None),
    )
    return jax.shard_map(
        local,
        mesh=mesh,
        in_specs=placed,
        out_specs=(P("layer", "row", "col", None), P(None, "layer")),
        check_vma=False,
    )
```

time: 199 us -> 35.5 us (0.18)
  blocking collectives: 71.9 us -> 0 us
  waiting for transfers between devices: 62 us -> 0 us
  Pallas kernels: 0 us -> 31.3 us
  between operations: 16.7 us -> 1.29 us
  matrix products: 14.8 us -> 0 us
  starting transfers between devices: 14.5 us -> 0 us
  other arithmetic: 12.3 us -> 0 us
  local copies, waits for them, and re-layouts: 5.32 us -> 2.73 us
    psum x4 -> x0, blocking collectives: 66.2 us -> none  [the longest x3 50.4 us: local(): lax.psum(jnp.sum(ranks_now / own_denominator, axis=(1, 2, 3)), ('row', 'c...]
    psum x4 -> x0, waiting for transfers between devices: 61.9 us -> none  [the longest x3 41.2 us: local(): whole = lax.psum(partial_value, 'col')]
    pallas_call x0 -> x1, Pallas kernels: none -> 31.3 us  [local(): pl.pallas_call(functools.partial(kernel, nl, nr, nc, nodes), out_shape=(j...]
    dot_general x8 -> x0, matrix products: 14.8 us -> none  [the longest x3 10.1 us: block_terms(): jnp.einsum('sij,sj->si', values, picked, preferred_element_type=jnp.float32)]
    ppermute x6 -> x0, starting transfers between devices: 14.3 us -> none  [the longest x3 10.4 us: with_halo(): before = lax.ppermute(last, axis, up)]
    reduce_sum x4 -> x0, other arithmetic: 7.89 us -> none  [the longest x3 5.25 us: local(): jnp.sum(ranks_now / own_denominator, axis=(1, 2, 3))]
    all_gather x3 -> x0, blocking collectives: 5.7 us -> none  [local(): column_vec = lax.all_gather(scaled_own, 'row', axis=1, tiled=True)]
    unnamed x8 -> x2, local copies, waits for them, and re-layouts: 0.02 us -> 2.73 us
  transfers between devices with their start and end apart: 10 -> 0, of which waited for: 4 -> 0; matrix products, arithmetic and copies ran while one was open for 0% -> 0% of each run, Pallas kernels for 0% -> 0%
where the time goes in v1:
time: 35.5 us; the launch traced here: 35.3 us
  Pallas kernels  31.3 us (88%)
  local copies, waits for them, and re-layouts  2.73 us (8%)
  between operations  1.29 us (4%)
    pallas_call x1, Pallas kernels, local(): pl.pallas_call(functools.partial(kernel, nl, nr, nc, nodes), out_shape=(j...  31.3 us
    unnamed x2, local copies, waits for them, and re-layouts  2.73 us

profile of v1, /device:TPU:0, one launch (start us, length us, event | category | flops | bytes accessed | tf_op | source)
XLA Modules:
  0.0 35.3 jit_solution(7644596476148635383)
XLA Ops:
  1.3 31.3 %shard_map.77 = (f32[128,128]{1,0:T(8,128)}, f32[3,1]{1,0:T(4,128)}) custom-call(bf16[32,256,256]{2,1,0:T(8,128)(2,1)} %bitcast.8, s32[1,32]{1,0:T(1,128)} %bitcast.12, s32[1,32]{1,0:T(1,128)} %bitcast.13, s32[1]{0:T(128)} %bitcast.7.count_ref, s32[128,128]{1,0:T(8,128)} %bitcast.9, f32[128,128]{1,0:T(8,128)} %bitcast.10), custom_call_target="tpu_custom_call" | custom-call | tf_op jit(solution)/shard_map/pallas_call | solution.py:377
  32.5 1.3 %copy.8 = f32[3,1]{0,1:T(1,128)} copy(f32[3,1]{1,0:T(4,128)} %get-tuple-element.7) | data formatting | bytes 24
  33.8 1.5 %copy.11 = f32[1,1,1,16384]{3,2,1,0:T(1,128)} copy(f32[1,1,1,16384]{3,2,1,0:T(1,128)} %bitcast.11) | data formatting | bytes 131072

commit v2 on v1

--- a/solution.py
+++ b/solution.py
@@ -36,13 +36,13 @@
     nl, nr, nc, nodes,
     values_hbm, rows_ref, cols_ref, count_ref, dang_hbm, start_hbm,
     ranks_hbm, resid_ref,
-    values, dang_in, start_in, out_buf, x_ref, inv_ref, kinv_ref, keep_ref,
+    values, dang_in, start_in, out_buf, x_ref, inv_ref, kinv_ref,
     colsum, ohrow, ohcol, own_prod, chg,
-    deg_send, deg_recv, row_send, row_recv,
+    px_recv, pd_recv, col_send, col_recv, cs_recv, row_send, row_recv,
     sc_send, sc_recv, ma_send, ma_recv, mb_send, mb_recv,
     pr_send, pr_recv, sp_send, sp_recv, rs_send, rs_recv,
     sem_in, sem_v,
-    deg_ss, deg_rs, row_ss, row_rs, sc_ss, sc_rs, ma_ss, ma_rs, mb_ss, mb_rs,
+    px_ss, px_rs, pd_ss, pd_rs, col_ss, col_rs, cs_ss, cs_rs, row_ss, row_rs, sc_ss, sc_rs, ma_ss, ma_rs, mb_ss, mb_rs,
     pr_ss, pr_rs, sp_ss, sp_rs, rs_ss, rs_rs,
 ):
     l, r, c = (lax.axis_index(a) for a in ("layer", "row", "col"))
@@ -66,10 +66,10 @@
         )
         for k in range(nchunk)
     ]
+    in_x.start()
+    in_d.start()
     for cp in vcopies:
         cp.start()
-    in_x.start()
-    in_d.start()
 
     peers = [(dr, dc) for dr in range(nr) for dc in range(nc) if (dr, dc) != (0, 0)]
     barrier = pltpu.get_barrier_semaphore()
@@ -95,6 +95,9 @@
     cols = jnp.where(live, cols_ref[...], -1)
     row_send[...] = jnp.broadcast_to(
         jnp.concatenate([rows, jnp.full((1, 128 - slots), -1, jnp.int32)], axis=1), (8, 128)
+    ).astype(f32)
+    col_send[...] = jnp.broadcast_to(
+        jnp.concatenate([cols, jnp.full((1, 128 - slots), -1, jnp.int32)], axis=1), (8, 128)
     ).astype(f32)
 
     eye = lax.broadcasted_iota(jnp.int32, (slots, slots), 0) == lax.broadcasted_iota(
@@ -110,42 +113,44 @@
 
     ones = jnp.ones((CHUNK, edge), bf16)
     rid = lax.broadcasted_iota(jnp.int32, (CHUNK, edge), 0)
-    for k in range(nchunk):
+
+    def column_sum(k):
         vcopies[k].wait()
         acc = jnp.zeros((CHUNK, edge), f32)
         for s in range(CHUNK):
             acc = jnp.where(rid == s, dot(ones, values[k * CHUNK + s]), acc)
-        colsum[k * CHUNK : (k + 1) * CHUNK] = acc
+        colsum[k] = acc
 
     in_x.wait()
     in_d.wait()
     for h in range(halves):
         x_ref[:, h * 128 : (h + 1) * 128] = start_in[pl.ds(h, blocks, stride=halves), :]
-        keep_ref[:, h * 128 : (h + 1) * 128] = 1.0 - dang_in[
-            pl.ds(h, blocks, stride=halves), :].astype(f32)
-
-    hi, lo = split(colsum[...])
-
-    def deg_of(rr):
-        base = rr * blocks
-        at = lax.broadcasted_iota(jnp.int32, (blocks, slots), 0) + base
-        oh = jnp.where(jnp.broadcast_to(cols, (blocks, slots)) == at, 1.0, 0.0).astype(bf16)
-        return dot(oh, hi) + dot(oh, lo)
-
-    for d in range(1, nr):
-        deg_send[d] = deg_of(lax.rem(r + d, nr))
+    column_sum(0)
+
+    order = []
+    first, last = jnp.int32(0), jnp.int32(nc - 1)
+    for _ in range(nc - 1):
+        left = (c - first >= last - c).astype(jnp.int32)
+        order.append(left * first + (1 - left) * last)
+        first, last = first + left, last - (1 - left)
+    far = [(cc, lax.rem(cc - c + nc, nc)) for cc in order]
 
     pl.semaphore_wait(
         barrier, len(peers) + (l > 0).astype(jnp.int32) + (l < nl - 1).astype(jnp.int32))
 
-    pre = []
+    px, pd, pc, pcs, prow = [], [], [], [], []
     for d in range(1, nr):
-        pre.append(remote(deg_send.at[d], deg_recv.at[d], deg_ss.at[d], deg_rs.at[d],
-                          l, lax.rem(r + d, nr), c))
-    for d in range(1, nc):
-        pre.append(remote(row_send, row_recv.at[d], row_ss.at[d], row_rs.at[d],
-                          l, r, lax.rem(c + d, nc)))
-    for cp in pre:
+        rr = lax.rem(r + d, nr)
+        px.append(remote(start_in, px_recv.at[d], px_ss.at[d], px_rs.at[d], l, rr, c))
+        pd.append(remote(dang_in, pd_recv.at[d], pd_ss.at[d], pd_rs.at[d], l, rr, c))
+        pc.append(remote(col_send, col_recv.at[d], col_ss.at[d], col_rs.at[d], l, rr, c))
+        pcs.append([
+            remote(colsum.at[k], cs_recv.at[d, k], cs_ss.at[d, k], cs_rs.at[d, k], l, rr, c)
+            for k in range(nchunk)
+        ])
+    for cc, d in far:
+        prow.append(remote(row_send, row_recv.at[d], row_ss.at[d], row_rs.at[d], l, r, cc))
+    for cp in px + pd + pc + prow + [q[0] for q in pcs]:
         cp.start()
 
     def spill_copies(t):
@@ -180,30 +185,59 @@
 
     send_spill(0, x_ref[...])
 
-    deg = deg_of(r)
-    for d in range(1, nr):
-        pre[d - 1].wait_recv()
-        deg = deg + deg_recv[d]
-    keep = keep_ref[...]
-    inv = 1.0 / (keep * deg + 1.0)
-    inv_ref[...] = inv
-    kinv_ref[...] = keep * inv
+    for k in range(1, nchunk):
+        column_sum(k)
+        for q in pcs:
+            q[k].start()
+
+    def spread_sums(tab, sums, rr):
+        at = (lax.broadcasted_iota(jnp.int32, (blocks, slots), 0) + rr * blocks).astype(f32)
+        oh = jnp.where(
+            jnp.broadcast_to(tab[0:1, 0:slots], (blocks, slots)) == at, 1.0, 0.0).astype(bf16)
+        hi, lo = split(sums.reshape(slots, edge))
+        return dot(oh, hi) + dot(oh, lo)
+
+    def piece(buf, h):
+        return buf[pl.ds(h, blocks, stride=halves), :]
+
+    near = [spread_sums(col_send, colsum[...], lax.rem(r - d + nr, nr)) for d in range(nr)]
+    for cp in px + pd + pc:
+        cp.wait_recv()
+    peer_x = {d: jnp.concatenate([piece(px_recv.at[d], h) for h in range(halves)], axis=1)
+              for d in range(1, nr)}
+    keeps = {d: 1.0 - jnp.concatenate(
+        [piece(pd_recv.at[d] if d else dang_in, h) for h in range(halves)], axis=1).astype(f32)
+        for d in range(nr)}
+    for q in pcs:
+        for cp in q:
+            cp.wait_recv()
+    for d in range(nr):
+        deg = near[d]
+        for e in range(1, nr):
+            deg = deg + spread_sums(col_recv[e], cs_recv[e], lax.rem(r - d + nr, nr))
+        inv = 1.0 / (keeps[d] * deg + 1.0)
+        kinv = keeps[d] * inv
+        if d == 0:
+            inv_ref[...] = inv
+            kinv_ref[...] = kinv
+        else:
+            sc_recv[0, d] = (peer_x[d] * kinv).astype(bf16)
 
     def row_onehot(tab):
         at = (lax.broadcasted_iota(jnp.int32, (blocks, slots), 0) + c * blocks).astype(f32)
         return jnp.where(jnp.broadcast_to(tab[0:1, 0:slots], (blocks, slots)) == at,
                          1.0, 0.0).astype(bf16)
 
-    chg[...] = jnp.zeros((8, 128), f32)
-
-    def step(t, _):
+    def step(t):
         x = x_ref[...]
         scaled = (x * kinv_ref[...]).astype(bf16)
-        sc_send[t] = scaled
+        if t > 0:
+            sc_send[t] = scaled
         sc = [
             remote(sc_send.at[t], sc_recv.at[t, d], sc_ss.at[t, d], sc_rs.at[t, d],
                    l, lax.rem(r + d, nr), c)
             for d in range(1, nr)
+            if t > 0
         ]
         for cp in sc:
             cp.start()
@@ -217,13 +251,13 @@
         for cp in ma:
             cp.start()
 
-        @pl.when(t > 0)
-        def _():
-            send_spill(t, x_ref[...])
+        if t > 0:
+            send_spill(t, x)
 
         picked = dot(ohcol[0], scaled)
         for d in range(1, nr):
-            sc[d - 1].wait_recv()
+            if t > 0:
+                sc[d - 1].wait_recv()
             picked = picked + dot(ohcol[d], sc_recv[t, d])
         picked = picked.astype(bf16)
 
@@ -238,11 +272,11 @@
                 acc = jnp.where(rid == s, res, acc)
             own_prod[k * CHUNK : (k + 1) * CHUNK] = acc
             pr_send[t, k] = acc.astype(pr_send.dtype)
-            for d in range(1, nc):
+            for cc, d in far:
                 cp = remote(pr_send.at[t, k], pr_recv.at[t, d, k], pr_ss.at[t, d, k],
-                            pr_rs.at[t, d, k], l, r, lax.rem(c + d, nc))
+                            pr_rs.at[t, d, k], l, r, cc)
                 cp.start()
-                pr.append((d, k, cp))
+                pr.append(cp)
 
         mass_row = mass_own
         for d in range(1, nr):
@@ -251,17 +285,17 @@
         mb_send[t] = mass_row
         mb = [
             remote(mb_send.at[t], mb_recv.at[t, d], mb_ss.at[t, d], mb_rs.at[t, d],
-                   l, r, lax.rem(c + d, nc))
-            for d in range(1, nc)
+                   l, r, cc)
+            for cc, d in far
         ]
         for cp in mb:
             cp.start()
 
-        @pl.when(t == 0)
-        def _():
+        if t == 0:
             ohrow[0] = row_onehot(row_send)
+            for cp in prow:
+                cp.wait_recv()
             for d in range(1, nc):
-                pre[nr - 1 + d - 1].wait_recv()
                 ohrow[d] = row_onehot(row_recv[d])
 
         phi, plo = split(own_prod[...])
@@ -279,12 +313,13 @@
 
         arrive = sp_recv[t, 0].astype(f32) + sp_recv[t, 1].astype(f32)
         mass = mass_row
+        for cp in mb:
+            cp.wait_recv()
         for d in range(1, nc):
-            mb[d - 1].wait_recv()
             mass = mass + mb_recv[t, d]
         rest = damping * ((1.0 - coupling) * (jnp.sum(mass) / nodes) + arrive) + (1.0 - damping)
 
-        for d, k, cp in pr:
+        for cp in pr:
             cp.wait_recv()
         for d in range(1, nc):
             got = pr_recv[t, d].reshape(slots, edge)
@@ -295,11 +330,9 @@
                 walk = walk + dot(ohrow[d], ghi) + dot(ohrow[d], glo)
         updated = damping * (1.0 - coupling) * walk + rest
         x_ref[...] = updated
-        change = jnp.sum(fold(jnp.abs(updated - x)))
-        lane = lax.broadcasted_iota(jnp.int32, (8, 128), 1)
-        chg[...] = jnp.where(lane == t, change, chg[...])
-
-        for cp in sc + ma + mb + [p[2] for p in pr]:
+        chg[t] = fold(jnp.abs(updated - x))
+
+        for cp in sc + ma + mb + pr:
             cp.wait_send()
 
         @pl.when(l < nl - 1)
@@ -310,11 +343,14 @@
         def _():
             down.wait_send()
 
-        return 0
-
-    lax.fori_loop(0, ITERS, step, 0)
-
-    rs_send[...] = chg[0:1]
+    for t in range(ITERS):
+        step(t)
+
+    lane = lax.broadcasted_iota(jnp.int32, (1, 128), 1)
+    changes = jnp.zeros((1, 128), f32)
+    for t in range(ITERS):
+        changes = jnp.where(lane == t, jnp.sum(chg[t]), changes)
+    rs_send[...] = changes
     rs = []
     for i, (dr, dc) in enumerate(peers):
         cp = remote(rs_send, rs_recv.at[i], rs_ss.at[i], rs_rs.at[i],
@@ -325,19 +361,21 @@
         out_buf[pl.ds(h, blocks, stride=halves), :] = x_ref[:, h * 128 : (h + 1) * 128]
     out = pltpu.make_async_copy(out_buf, ranks_hbm, sem_in.at[0])
     out.start()
-    for cp in pre:
+    for cp in px + pd + pc + prow + [e for q in pcs for e in q]:
         cp.wait_send()
     total = rs_send[...]
     for i, cp in enumerate(rs):
         cp.wait_recv()
         total = total + rs_recv[i]
-    pick = lax.broadcasted_iota(jnp.int32, (ITERS, 128), 0) == lax.broadcasted_iota(
-        jnp.int32, (ITERS, 128), 1)
-    resid_ref[...] = jnp.sum(
-        jnp.where(pick, jnp.broadcast_to(total, (ITERS, 128)), 0.0), axis=1, keepdims=True)
+    resid_ref[...] = total
     for cp in rs:
         cp.wait_send()
     out.wait()
+
+
+def finish(ranks_in, resid_in, ranks_ref, resid_ref):
+    ranks_ref[...] = ranks_in[...]
+    resid_ref[...] = resid_in[:, 0:ITERS]
 
 
 def local(block_values, block_rows, block_cols, block_count, dangling, start_ranks):
@@ -354,10 +392,12 @@
     PT, ST = bf16, f32
     scratch = [
         vm((slots, edge, edge), bf16), vm((span // 128, 128), jnp.int32), vm((span // 128, 128), f32),
-        vm((span // 128, 128), f32), vm(big, f32), vm(big, f32), vm(big, f32), vm(big, f32),
-        vm((slots, edge), f32), vm((nc, blocks, slots), bf16), vm((nr, slots, blocks), bf16),
-        vm((slots, edge), f32), vm((8, 128), f32),
-        vm((nr,) + big, f32), vm((nr,) + big, f32), vm((8, 128), f32), vm((nc, 8, 128), f32),
+        vm((span // 128, 128), f32), vm(big, f32), vm(big, f32), vm(big, f32),
+        vm((nchunk, CHUNK, edge), f32), vm((nc, blocks, slots), bf16), vm((nr, slots, blocks), bf16),
+        vm((slots, edge), f32), vm((ITERS, 8, 128), f32),
+        vm((nr, span // 128, 128), f32), vm((nr, span // 128, 128), jnp.int32),
+        vm((8, 128), f32), vm((nr, 8, 128), f32), vm((nr, nchunk, CHUNK, edge), f32),
+        vm((8, 128), f32), vm((nc, 8, 128), f32),
         vm((ITERS,) + big, bf16), vm((ITERS, nr) + big, bf16),
         vm((ITERS, 8, 128), f32), vm((ITERS, nr, 8, 128), f32),
         vm((ITERS, 8, 128), f32), vm((ITERS, nc, 8, 128), f32),
@@ -365,7 +405,8 @@
         vm((ITERS,) + big, ST), vm((ITERS, 2) + big, ST),
         vm((1, 128), f32), vm((npeer, 1, 128), f32),
         dma((2,)), dma((nchunk,)),
-        dma((nr,)), dma((nr,)), dma((nc,)), dma((nc,)),
+        dma((nr,)), dma((nr,)), dma((nr,)), dma((nr,)), dma((nr,)), dma((nr,)),
+        dma((nr, nchunk)), dma((nr, nchunk)), dma((nc,)), dma((nc,)),
         dma((ITERS, nr)), dma((ITERS, nr)), dma((ITERS, nr)), dma((ITERS, nr)),
         dma((ITERS, nc)), dma((ITERS, nc)),
         dma((ITERS, nc, nchunk)), dma((ITERS, nc, nchunk)),
@@ -378,7 +419,7 @@
         functools.partial(kernel, nl, nr, nc, nodes),
         out_shape=(
             jax.ShapeDtypeStruct((span // 128, 128), f32),
-            jax.ShapeDtypeStruct((ITERS, 1), f32),
+            jax.ShapeDtypeStruct((1, 128), f32),
         ),
         in_specs=[hbm, vmem, vmem, smem, hbm, hbm],
         out_specs=(hbm, vmem),
@@ -392,7 +433,16 @@
         dangling.reshape(span // 128, 128),
         start_ranks.reshape(span // 128, 128),
     )
-    return ranks.reshape(1, 1, 1, span), resid
+    ranks, resid = pl.pallas_call(
+        finish,
+        out_shape=(
+            jax.ShapeDtypeStruct((span // 128, 128), f32),
+            jax.ShapeDtypeStruct((1, ITERS), f32),
+        ),
+        in_specs=[vmem, vmem],
+        out_specs=(vmem, vmem),
+    )(ranks, resid)
+    return ranks.reshape(1, 1, 1, span), resid.T
 
 
 def solution(mesh):

time: 35.5 us -> 33.7 us (0.949)
  local copies, waits for them, and re-layouts: 2.73 us -> 0 us
  Pallas kernels: 31.3 us -> 32.2 us
    unnamed x2 -> x0, local copies, waits for them, and re-layouts: 2.73 us -> none
    pallas_call x0 -> x1, Pallas kernels: none -> 1.48 us  [local(): pl.pallas_call(finish, out_shape=(jax.ShapeDtypeStruct((span // 128, 128)...]
    pallas_call x1, Pallas kernels: 31.3 us -> 30.7 us  [local(): pl.pallas_call(functools.partial(kernel, nl, nr, nc, nodes), out_shape=(j...]
where the time goes in v2:
time: 33.7 us; the launch traced here: 33.5 us
  Pallas kernels  32.2 us (96%)
  between operations  1.28 us (4%)
    pallas_call x1, Pallas kernels, local(): pl.pallas_call(functools.partial(kernel, nl, nr, nc, nodes), out_shape=(j...  30.7 us
    pallas_call x1, Pallas kernels, local(): pl.pallas_call(finish, out_shape=(jax.ShapeDtypeStruct((span // 128, 128)...  1.48 us

profile of v2, /device:TPU:0, one launch (start us, length us, event | category | flops | bytes accessed | tf_op | source)
XLA Modules:
  0.0 33.5 jit_solution(9887866390510183471)
XLA Ops:
  1.3 30.7 %shard_map.77 = (f32[128,128]{1,0:T(8,128)}, f32[1,128]{1,0:T(1,128)}) custom-call(bf16[32,256,256]{2,1,0:T(8,128)(2,1)} %bitcast.9, s32[1,32]{1,0:T(1,128)} %bitcast.12, s32[1,32]{1,0:T(1,128)} %bitcast.13, s32[1]{0:T(128)} %bitcast.8.count_ref, s32[128,128]{1,0:T(8,128)} %bitcast.10, f32[128,128]{1,0:T(8,128)} %bitcast.11), custom_call_target="tpu_custom_call" | custom-call | tf_op jit(solution)/shard_map/pallas_call | solution.py:418
  32.0 1.5 %shard_map.78 = (f32[128,128]{1,0:T(8,128)}, f32[1,3]{1,0:T(1,128)}) custom-call(f32[128,128]{1,0:T(8,128)} %get-tuple-element.6.ranks_in, f32[1,128]{1,0:T(1,128)} %get-tuple-element.7.resid_in), custom_call_target="tpu_custom_call" | custom-call | tf_op jit(solution)/shard_map/pallas_call | solution.py:436

commit v3 on v2

--- a/solution.py
+++ b/solution.py
@@ -35,14 +35,14 @@
 def kernel(
     nl, nr, nc, nodes,
     values_hbm, rows_ref, cols_ref, count_ref, dang_hbm, start_hbm,
-    ranks_hbm, resid_ref,
-    values, dang_in, start_in, out_buf, x_ref, inv_ref, kinv_ref,
+    ranks_ref, resid_ref,
+    values, dang_in, start_in, x_ref, inv_ref, kinv_ref,
     colsum, ohrow, ohcol, own_prod, chg,
     px_recv, pd_recv, col_send, col_recv, cs_recv, row_send, row_recv,
-    sc_send, sc_recv, ma_send, ma_recv, mb_send, mb_recv,
+    sc_send, sc_recv, ma_send, ma_recv,
     pr_send, pr_recv, sp_send, sp_recv, rs_send, rs_recv,
     sem_in, sem_v,
-    px_ss, px_rs, pd_ss, pd_rs, col_ss, col_rs, cs_ss, cs_rs, row_ss, row_rs, sc_ss, sc_rs, ma_ss, ma_rs, mb_ss, mb_rs,
+    px_ss, px_rs, pd_ss, pd_rs, col_ss, col_rs, cs_ss, cs_rs, row_ss, row_rs, sc_ss, sc_rs, ma_ss, ma_rs,
     pr_ss, pr_rs, sp_ss, sp_rs, rs_ss, rs_rs,
 ):
     l, r, c = (lax.axis_index(a) for a in ("layer", "row", "col"))
@@ -134,6 +134,9 @@
         order.append(left * first + (1 - left) * last)
         first, last = first + left, last - (1 - left)
     far = [(cc, lax.rem(cc - c + nc, nc)) for cc in order]
+    far_peers = [(dr, cc, d) for cc, d in far for dr in range(nr)]
+    far_peers += [(dr, c, 0) for dr in range(1, nr)]
+    sent = []
 
     pl.semaphore_wait(
         barrier, len(peers) + (l > 0).astype(jnp.int32) + (l < nl - 1).astype(jnp.int32))
@@ -241,13 +244,13 @@
         ]
         for cp in sc:
             cp.start()
-        mass_own = fold(x * inv_ref[...])
+        mass_own = jnp.sum(fold(x * inv_ref[...]), axis=0, keepdims=True)
         ma_send[t] = mass_own
-        ma = [
-            remote(ma_send.at[t], ma_recv.at[t, d], ma_ss.at[t, d], ma_rs.at[t, d],
-                   l, lax.rem(r + d, nr), c)
-            for d in range(1, nr)
-        ]
+        ma = []
+        for i, (dr, cc, dc) in enumerate(far_peers):
+            slot = dr * nc + dc - 1
+            ma.append(remote(ma_send.at[t], ma_recv.at[t, slot], ma_ss.at[t, slot],
+                             ma_rs.at[t, slot], l, lax.rem(r + dr, nr), cc))
         for cp in ma:
             cp.start()
 
@@ -278,19 +281,6 @@
                 cp.start()
                 pr.append(cp)
 
-        mass_row = mass_own
-        for d in range(1, nr):
-            ma[d - 1].wait_recv()
-            mass_row = mass_row + ma_recv[t, d]
-        mb_send[t] = mass_row
-        mb = [
-            remote(mb_send.at[t], mb_recv.at[t, d], mb_ss.at[t, d], mb_rs.at[t, d],
-                   l, r, cc)
-            for cc, d in far
-        ]
-        for cp in mb:
-            cp.start()
-
         if t == 0:
             ohrow[0] = row_onehot(row_send)
             for cp in prow:
@@ -312,11 +302,11 @@
             down.wait_recv()
 
         arrive = sp_recv[t, 0].astype(f32) + sp_recv[t, 1].astype(f32)
-        mass = mass_row
-        for cp in mb:
+        mass = mass_own
+        for cp in ma:
             cp.wait_recv()
-        for d in range(1, nc):
-            mass = mass + mb_recv[t, d]
+        for i in range(len(peers)):
+            mass = mass + ma_recv[t, i]
         rest = damping * ((1.0 - coupling) * (jnp.sum(mass) / nodes) + arrive) + (1.0 - damping)
 
         for cp in pr:
@@ -332,16 +322,7 @@
         x_ref[...] = updated
         chg[t] = fold(jnp.abs(updated - x))
 
-        for cp in sc + ma + mb + pr:
-            cp.wait_send()
-
-        @pl.when(l < nl - 1)
-        def _():
-            up.wait_send()
-
-        @pl.when(l > 0)
-        def _():
-            down.wait_send()
+        sent.extend(sc + ma + pr)
 
     for t in range(ITERS):
         step(t)
@@ -358,11 +339,21 @@
         cp.start()
         rs.append(cp)
     for h in range(halves):
-        out_buf[pl.ds(h, blocks, stride=halves), :] = x_ref[:, h * 128 : (h + 1) * 128]
-    out = pltpu.make_async_copy(out_buf, ranks_hbm, sem_in.at[0])
-    out.start()
-    for cp in px + pd + pc + prow + [e for q in pcs for e in q]:
+        ranks_ref[pl.ds(h, blocks, stride=halves), :] = x_ref[:, h * 128 : (h + 1) * 128]
+    for cp in px + pd + pc + prow + [e for q in pcs for e in q] + sent:
         cp.wait_send()
+    ups = [spill_copies(t) for t in range(ITERS)]
+
+    @pl.when(l < nl - 1)
+    def _():
+        for up, _ in ups:
+            up.wait_send()
+
+    @pl.when(l > 0)
+    def _():
+        for _, down in ups:
+            down.wait_send()
+
     total = rs_send[...]
     for i, cp in enumerate(rs):
         cp.wait_recv()
@@ -370,7 +361,6 @@
     resid_ref[...] = total
     for cp in rs:
         cp.wait_send()
-    out.wait()
 
 
 def finish(ranks_in, resid_in, ranks_ref, resid_ref):
@@ -392,37 +382,35 @@
     PT, ST = bf16, f32
     scratch = [
         vm((slots, edge, edge), bf16), vm((span // 128, 128), jnp.int32), vm((span // 128, 128), f32),
-        vm((span // 128, 128), f32), vm(big, f32), vm(big, f32), vm(big, f32),
+        vm(big, f32), vm(big, f32), vm(big, f32),
         vm((nchunk, CHUNK, edge), f32), vm((nc, blocks, slots), bf16), vm((nr, slots, blocks), bf16),
         vm((slots, edge), f32), vm((ITERS, 8, 128), f32),
         vm((nr, span // 128, 128), f32), vm((nr, span // 128, 128), jnp.int32),
         vm((8, 128), f32), vm((nr, 8, 128), f32), vm((nr, nchunk, CHUNK, edge), f32),
         vm((8, 128), f32), vm((nc, 8, 128), f32),
         vm((ITERS,) + big, bf16), vm((ITERS, nr) + big, bf16),
-        vm((ITERS, 8, 128), f32), vm((ITERS, nr, 8, 128), f32),
-        vm((ITERS, 8, 128), f32), vm((ITERS, nc, 8, 128), f32),
+        vm((ITERS, 1, 128), f32), vm((ITERS, npeer, 1, 128), f32),
         vm((ITERS, nchunk, CHUNK, edge), PT), vm((ITERS, nc, nchunk, CHUNK, edge), PT),
         vm((ITERS,) + big, ST), vm((ITERS, 2) + big, ST),
         vm((1, 128), f32), vm((npeer, 1, 128), f32),
         dma((2,)), dma((nchunk,)),
         dma((nr,)), dma((nr,)), dma((nr,)), dma((nr,)), dma((nr,)), dma((nr,)),
         dma((nr, nchunk)), dma((nr, nchunk)), dma((nc,)), dma((nc,)),
-        dma((ITERS, nr)), dma((ITERS, nr)), dma((ITERS, nr)), dma((ITERS, nr)),
-        dma((ITERS, nc)), dma((ITERS, nc)),
+        dma((ITERS, nr)), dma((ITERS, nr)), dma((ITERS, npeer)), dma((ITERS, npeer)),
         dma((ITERS, nc, nchunk)), dma((ITERS, nc, nchunk)),
         dma((ITERS, 2)), dma((ITERS, 2)), dma((npeer,)), dma((npeer,)),
     ]
-    hbm = pl.BlockSpec(memory_space=pl.ANY)
+    hbm = pl.BlockSpec(memory_space=pltpu.HBM)
     vmem = pl.BlockSpec(memory_space=pltpu.VMEM)
     smem = pl.BlockSpec(memory_space=pltpu.SMEM)
     ranks, resid = pl.pallas_call(
         functools.partial(kernel, nl, nr, nc, nodes),
         out_shape=(
-            jax.ShapeDtypeStruct((span // 128, 128), f32),
-            jax.ShapeDtypeStruct((1, 128), f32),
+            pltpu.VMEM((span // 128, 128), f32),
+            pltpu.VMEM((1, 128), f32),
         ),
         in_specs=[hbm, vmem, vmem, smem, hbm, hbm],
-        out_specs=(hbm, vmem),
+        out_specs=(vmem, vmem),
         scratch_shapes=scratch,
         compiler_params=pltpu.CompilerParams(collective_id=0, has_side_effects=True),
     )(
@@ -441,6 +429,7 @@
         ),
         in_specs=[vmem, vmem],
         out_specs=(vmem, vmem),
+        compiler_params=pltpu.CompilerParams(vmem_limit_bytes=4 * 1024 * 1024),
     )(ranks, resid)
     return ranks.reshape(1, 1, 1, span), resid.T
 

time: 33.7 us -> 30.7 us (0.911)
  Pallas kernels: 32.2 us -> 29.2 us
    pallas_call x1, Pallas kernels: 30.7 us -> 28.6 us  [local(): pl.pallas_call(functools.partial(kernel, nl, nr, nc, nodes), out_shape=(p...]
    pallas_call x1, Pallas kernels: 1.48 us -> 0.64 us  [local(): pl.pallas_call(finish, out_shape=(jax.ShapeDtypeStruct((span // 128, 128)...]
where the time goes in v3:
time: 30.7 us; the launch traced here: 30.5 us
  Pallas kernels  29.2 us (95%)
  between operations  1.28 us (4%)
    pallas_call x1, Pallas kernels, local(): pl.pallas_call(functools.partial(kernel, nl, nr, nc, nodes), out_shape=(p...  28.6 us
    pallas_call x1, Pallas kernels, local(): pl.pallas_call(finish, out_shape=(jax.ShapeDtypeStruct((span // 128, 128)...  0.64 us

profile of v3, /device:TPU:0, one launch (start us, length us, event | category | flops | bytes accessed | tf_op | source)
XLA Modules:
  0.0 30.5 jit_solution(9116236717751763874)
XLA Ops:
  1.3 28.6 %shard_map.77 = (f32[128,128]{1,0:T(8,128)S(1)}, f32[1,128]{1,0:T(1,128)S(1)}) custom-call(bf16[32,256,256]{2,1,0:T(8,128)(2,1)} %bitcast.9, s32[1,32]{1,0:T(1,128)} %bitcast.12, s32[1,32]{1,0:T(1,128)} %bitcast.13, s32[1]{0:T(128)} %bitcast.8.count_ref, s32[128,128]{1,0:T(8,128)} %bitcast.10, f32[128,128]{1,0:T(8,128)} %bitcast.11), custom_call_target="tpu_custom_call" | custom-call | tf_op jit(solution)/shard_map/pallas_call | solution.py:406
  29.9 0.6 %shard_map.78 = (f32[128,128]{1,0:T(8,128)}, f32[1,3]{1,0:T(1,128)}) custom-call(f32[128,128]{1,0:T(8,128)S(1)} %get-tuple-element.6.ranks_in, f32[1,128]{1,0:T(1,128)S(1)} %get-tuple-element.7.resid_in), custom_call_target="tpu_custom_call" | custom-call | tf_op jit(solution)/shard_map/pallas_call | solution.py:424

commit v4 on v3

--- a/solution.py
+++ b/solution.py
@@ -90,7 +90,7 @@
         pl.semaphore_signal(
             barrier, inc=1, device_id=(l + 1, r, c), device_id_type=pl.DeviceIdType.MESH)
 
-    live = lax.broadcasted_iota(jnp.int32, (1, slots), 1) < count_ref[0]
+    live = lax.broadcasted_iota(jnp.int32, (1, slots), 1) < count_ref[...]
     rows = jnp.where(live, rows_ref[...], -1)
     cols = jnp.where(live, cols_ref[...], -1)
     row_send[...] = jnp.broadcast_to(
@@ -309,9 +309,9 @@
             mass = mass + ma_recv[t, i]
         rest = damping * ((1.0 - coupling) * (jnp.sum(mass) / nodes) + arrive) + (1.0 - damping)
 
-        for cp in pr:
-            cp.wait_recv()
         for d in range(1, nc):
+            for k in range(nchunk):
+                remote(pr_send.at[t, k], pr_recv.at[t, d, k], pr_ss.at[t, d, k], pr_rs.at[t, d, k], l, r, lax.rem(c + d, nc)).wait_recv()
             got = pr_recv[t, d].reshape(slots, edge)
             if got.dtype == bf16:
                 walk = walk + dot(ohrow[d], got)
@@ -333,9 +333,10 @@
         changes = jnp.where(lane == t, jnp.sum(chg[t]), changes)
     rs_send[...] = changes
     rs = []
-    for i, (dr, dc) in enumerate(peers):
+    for dr, cc, dc in far_peers:
+        i = dr * nc + dc - 1
         cp = remote(rs_send, rs_recv.at[i], rs_ss.at[i], rs_rs.at[i],
-                    l, lax.rem(r + dr, nr), lax.rem(c + dc, nc))
+                    l, lax.rem(r + dr, nr), cc)
         cp.start()
         rs.append(cp)
     for h in range(halves):
@@ -355,8 +356,9 @@
             down.wait_send()
 
     total = rs_send[...]
-    for i, cp in enumerate(rs):
+    for cp in rs:
         cp.wait_recv()
+    for i in range(len(peers)):
         total = total + rs_recv[i]
     resid_ref[...] = total
     for cp in rs:
@@ -402,14 +404,13 @@
     ]
     hbm = pl.BlockSpec(memory_space=pltpu.HBM)
     vmem = pl.BlockSpec(memory_space=pltpu.VMEM)
-    smem = pl.BlockSpec(memory_space=pltpu.SMEM)
     ranks, resid = pl.pallas_call(
         functools.partial(kernel, nl, nr, nc, nodes),
         out_shape=(
             pltpu.VMEM((span // 128, 128), f32),
             pltpu.VMEM((1, 128), f32),
         ),
-        in_specs=[hbm, vmem, vmem, smem, hbm, hbm],
+        in_specs=[hbm, vmem, vmem, vmem, hbm, hbm],
         out_specs=(vmem, vmem),
         scratch_shapes=scratch,
         compiler_params=pltpu.CompilerParams(collective_id=0, has_side_effects=True),
@@ -417,7 +418,7 @@
         block_values.reshape(slots, edge, edge),
         block_rows.reshape(1, slots),
         block_cols.reshape(1, slots),
-        block_count.reshape(1),
+        block_count.reshape(1, 1),
         dangling.reshape(span // 128, 128),
         start_ranks.reshape(span // 128, 128),
     )

time: 30.7 us -> 30.6 us (level)
  no operation moved by 1% of the time
where the time goes in v4:
time: 30.6 us; the launch traced here: 30.4 us
  Pallas kernels  29.1 us (95%)
  between operations  1.28 us (4%)
    pallas_call x1, Pallas kernels, local(): pl.pallas_call(functools.partial(kernel, nl, nr, nc, nodes), out_shape=(p...  28.5 us
    pallas_call x1, Pallas kernels, local(): pl.pallas_call(finish, out_shape=(jax.ShapeDtypeStruct((span // 128, 128)...  0.64 us

profile of v4, /device:TPU:0, one launch (start us, length us, event | category | flops | bytes accessed | tf_op | source)
XLA Modules:
  0.0 30.4 jit_solution(6775174844861136523)
XLA Ops:
  1.3 28.5 %shard_map.77 = (f32[128,128]{1,0:T(8,128)S(1)}, f32[1,128]{1,0:T(1,128)S(1)}) custom-call(bf16[32,256,256]{2,1,0:T(8,128)(2,1)} %bitcast.9, s32[1,32]{1,0:T(1,128)} %bitcast.12, s32[1,32]{1,0:T(1,128)} %bitcast.13, s32[1,1]{1,0:T(1,128)} %bitcast.8.count_ref, s32[128,128]{1,0:T(8,128)} %bitcast.10, f32[128,128]{1,0:T(8,128)} %bitcast.11), custom_call_target="tpu_custom_call" | custom-call | tf_op jit(solution)/shard_map/pallas_call | solution.py:407
  29.8 0.6 %shard_map.78 = (f32[128,128]{1,0:T(8,128)}, f32[1,3]{1,0:T(1,128)}) custom-call(f32[128,128]{1,0:T(8,128)S(1)} %get-tuple-element.6.ranks_in, f32[1,128]{1,0:T(1,128)S(1)} %get-tuple-element.7.resid_in), custom_call_target="tpu_custom_call" | custom-call | tf_op jit(solution)/shard_map/pallas_call | solution.py:425
